TPU v7x, 32 devices: a whole 2x2x4 slice. The times are simulated.
32 devices in a mesh: dom: 32 (over z, y, x, core).
Axes of the slice: x: 2, y: 2, z: 4, core: 2. Of those that a mesh axis runs over, the one named last changes fastest.
Arguments:
- features: bfloat16 [32768, 256], P('dom'), may hold values from -6 to 6
- edge_source: int32 [32, 128, 128], P('dom'), may hold values from 0 to 2047, as said below
- edge_relation: int32 [32, 128, 128], P('dom'), may hold values from 0 to 7
- edge_target: int32 [32, 128, 128], P('dom'), may hold values from 0 to 1023, as said below
- block_count: int32 [32], P('dom'), may hold values from 1 to 128, as said below
- send_list: int32 [32, 32, 32], P('dom'), may hold values from 0 to 1023
- bases_first: bfloat16 [30, 256, 256], P(None, 'dom'), may hold values from -0.375 to 0.375
- self_first: bfloat16 [256, 256], P('dom'), may hold values from -0.375 to 0.375
- coef_first: float32 [8, 30], replicated, may hold values from -1 to 1
- bias_first: float32 [256], replicated, may hold values from -3 to 3
- bases_second: bfloat16 [30, 256, 256], P(None, 'dom'), may hold values from -0.375 to 0.375
- self_second: bfloat16 [256, 256], P('dom'), may hold values from -0.375 to 0.375
- coef_second: float32 [8, 30], replicated, may hold values from -1 to 1
- bias_second: float32 [256], replicated, may hold values from -3 to 3
Outputs:
- embedded: bfloat16 [32768, 256], P('dom')
Inputs may be any that keep to these rules, and one draw needn't show every extreme that they name: `edge_source`: an entry below 1024 names a row of the edge's own partition; an entry 1024 + p * 32 + s names the row that partition p sends to the edge's partition in slot s, and p is never the edge's own partition. `edge_target`: non-decreasing within each block; all targets of one block lie in one aligned window of 16 rows, from 16 * k to 16 * k + 15 for some k. `block_count`: blocks at and beyond it are ignored; some partition uses all 128.
All inputs are finite; a program needn't handle non-finite values.
Results may differ from a plain program's by a relative error of at most 0.0064.
Values may be sent and summed in bfloat16 or wider, within the bound.
A program may use at most 128 MiB of HBM per device.

v0:
```python
import functools
import math

import jax
import jax.numpy as jnp
from jax import lax
from jax.experimental import pallas as pl
from jax.experimental.pallas import tpu as pltpu
from jax.sharding import PartitionSpec as P

WIN = 16
VMEM_LIMIT = 40 * 1024 * 1024


def compose_weights(coef, bases):
    mixed = jnp.einsum(
        "rb,bij->rij", coef, bases.astype(jnp.float32), precision=lax.Precision.HIGHEST
    )
    return mixed.astype(jnp.bfloat16)


def weight_share(bases, self_weight, coef):
    local_mixed = compose_weights(coef, bases)
    return jnp.concatenate([local_mixed, self_weight[None]], axis=0)[:, None]


def digits_of(devices):
    chips = devices // 2
    side = max(math.isqrt(chips // 4), 1)
    sizes = (side, side, chips // (side * side))
    digits, stride = [], 2
    for size in sizes:
        digits.append((size, stride))
        stride *= size
    return digits


def shift_pairs(devices, radix, stride, hop):
    pairs = []
    for device in range(devices):
        digit = device // stride % radix
        pairs.append((device, device + ((digit + hop) % radix - digit) * stride))
    return pairs


def send_digit(share, devices, radix, stride):
    return [
        lax.ppermute(share, "dom", shift_pairs(devices, radix, stride, hop))
        for hop in range(1, radix)
    ]


def join_digit(share, came, radix, stride, inner=False):
    if radix == 1:
        return share
    digit = lax.axis_index("dom") // stride % radix
    place = 2 if inner else 1
    if radix == 2:
        low = digit == 0
        parts = [jnp.where(low, share, came[0]), jnp.where(low, came[0], share)]
        full = jnp.stack(parts, axis=place)
    else:
        full = jnp.stack([share] * radix, axis=place)
        for hop, piece in enumerate(came, start=1):
            start = [0] * full.ndim
            start[place] = lax.rem(digit + radix - hop, radix)
            full = lax.dynamic_update_slice(full, jnp.expand_dims(piece, place), start)
    return full.reshape(share.shape[0], share.shape[1] * radix, *share.shape[2:])


def gather_digit(share, devices, radix, stride, inner=False):
    return join_digit(share, send_digit(share, devices, radix, stride), radix, stride, inner)


def spread_rows(rows_ref, table_ref, base, parts):
    rows = rows_ref.shape[0]
    step = 256

    def body(chunk, carry):
        first = pl.multiple_of(chunk * step, step)
        for part in range(parts):
            values = rows_ref[pl.ds(first, step), part * 128 : (part + 1) * 128]
            table_ref[pl.ds((base + first) * parts + part, step, stride=parts), :] = values.astype(
                jnp.float32
            )
        return carry

    lax.fori_loop(0, rows // step, body, 0)


def pick_rows(list_ref, major, minor, count, table_ref, held_ref, parts):
    listed = list_ref.at[major]
    for row in range(count):
        source = listed[minor + row]
        held_ref[pl.ds(row * parts, parts), :] = table_ref[
            pl.ds(pl.multiple_of(source, parts), parts), :
        ]


def held_rows(held_ref, count, parts):
    return jnp.concatenate(
        [
            held_ref[pl.ds(part, count, stride=parts), :].astype(jnp.bfloat16)
            for part in range(parts)
        ],
        axis=1,
    )


def send_rows_out(send_ref, table_ref, held_a, held_b, out_ref, parts):
    peers, slots = send_ref.shape

    def body(pair, carry):
        for side, held in ((0, held_a), (1, held_b)):
            peer = pair * 2 + side
            pick_rows(send_ref, peer, 0, slots, table_ref, held, parts)
            out_ref[pl.ds(pl.multiple_of(peer * slots, slots), slots), :] = held_rows(
                held, slots, parts
            )
        return carry

    lax.fori_loop(0, peers // 2, body, 0)


def outgoing_kernel(send_ref, rows_ref, out_ref, table_ref, held_a, held_b):
    parts = rows_ref.shape[1] // 128
    spread_rows(rows_ref, table_ref, 0, parts)
    send_rows_out(send_ref, table_ref, held_a, held_b, out_ref, parts)


def pool_kernel(
    source_ref,
    window_ref,
    count_ref,
    slot_ref,
    own_ref,
    come_ref,
    mean_ref,
    table_ref,
    held_a,
    held_b,
    pooled_ref,
    degree_ref,
):
    node_rows, width = own_ref.shape
    parts = width // 128
    tiles, slots, _ = pooled_ref.shape
    relations = slots // WIN
    blocks, block_width = slot_ref.shape
    count = count_ref[0]

    spread_rows(own_ref, table_ref, 0, parts)
    spread_rows(come_ref, table_ref, node_rows, parts)

    def clear(tile, carry):
        pooled_ref[tile] = jnp.zeros(pooled_ref.shape[1:], jnp.float32)
        degree_ref[tile] = jnp.zeros(degree_ref.shape[1:], jnp.float32)
        return carry

    lax.fori_loop(0, tiles, clear, 0)

    slot_ids = lax.broadcasted_iota(jnp.int32, (slots, block_width), 0)
    ones = jnp.ones((block_width, 128), jnp.bfloat16)

    def pool(block, held):
        local = slot_ref[pl.ds(block, 1), :]
        local = jnp.where(block < count, local, -1)
        hot = (slot_ids == local).astype(jnp.float32).astype(jnp.bfloat16)
        sums = jnp.dot(
            hot, held_rows(held, block_width, parts), preferred_element_type=jnp.float32
        )
        numbers = jnp.dot(hot, ones, preferred_element_type=jnp.float32)
        window = window_ref[block]
        pooled_ref[window] += sums
        degree_ref[window] += numbers

    def gather(block, held):
        block = jnp.minimum(block, blocks - 1)
        pick_rows(source_ref, block, 0, block_width, table_ref, held, parts)

    gather(0, held_a)

    def body(pair, carry):
        block = pair * 2
        gather(block + 1, held_b)
        pool(block, held_a)
        gather(block + 2, held_a)
        pool(jnp.minimum(block + 1, blocks - 1), held_b)
        return carry

    lax.fori_loop(0, (count + 1) // 2, body, 0)

    def average(tile, carry):
        first = pl.multiple_of(tile * WIN, WIN)
        for relation in range(relations):
            rows = slice(relation * WIN, (relation + 1) * WIN)
            inverse = 1.0 / jnp.maximum(degree_ref[tile, rows, :], 1.0)
            for part in range(parts):
                lanes = slice(part * 128, (part + 1) * 128)
                mean_ref[relation, pl.ds(first, WIN), lanes] = (
                    pooled_ref[tile, rows, lanes] * inverse
                ).astype(jnp.bfloat16)
        return carry

    lax.fori_loop(0, tiles, average, 0)


def dense_kernel(last, *refs):
    if last:
        own_ref, mean_ref, weight_ref, bias_ref, out_ref = refs
    else:
        send_ref, own_ref, mean_ref, weight_ref, bias_ref, out_ref, sent_ref = refs[:7]
        table_ref, held_a, held_b = refs[7:]
    node_rows, width = own_ref.shape
    parts = width // 128
    relations = mean_ref.shape[0]
    bias = bias_ref[...]

    def dense(chunk, carry):
        rows = pl.ds(pl.multiple_of(chunk * 256, 256), 256)
        total = bias + jnp.dot(
            own_ref[rows, :], weight_ref[relations], preferred_element_type=jnp.float32
        )
        for relation in range(relations):
            total = total + jnp.dot(
                mean_ref[relation, rows, :],
                weight_ref[relation],
                preferred_element_type=jnp.float32,
            )
        if not last:
            total = jnp.maximum(total, 0.0)
        rounded = total.astype(jnp.bfloat16)
        out_ref[rows, :] = rounded
        if not last:
            for part in range(parts):
                table_ref[pl.ds(chunk * 256 * parts + part, 256, stride=parts), :] = rounded[
                    :, part * 128 : (part + 1) * 128
                ].astype(jnp.float32)
        return carry

    lax.fori_loop(0, node_rows // 256, dense, 0)
    if not last:
        send_rows_out(send_ref, table_ref, held_a, held_b, sent_ref, parts)


def exchange_kernel(devices, out_ref, in_ref, send_sems, recv_sems):
    me = lax.axis_index("dom")

    def copy_to(hop):
        peer = lax.rem(me + hop, devices)
        return pltpu.make_async_remote_copy(
            src_ref=out_ref.at[peer],
            dst_ref=in_ref.at[me],
            send_sem=send_sems.at[hop],
            recv_sem=recv_sems.at[hop],
            device_id=(peer,),
            device_id_type=pl.DeviceIdType.MESH,
        )

    def copy_from(hop):
        peer = lax.rem(me + devices - hop, devices)
        return pltpu.make_async_remote_copy(
            src_ref=out_ref.at[peer],
            dst_ref=in_ref.at[peer],
            send_sem=send_sems.at[hop],
            recv_sem=recv_sems.at[hop],
            device_id=(peer,),
            device_id_type=pl.DeviceIdType.MESH,
        )

    def start(hop, carry):
        copy_to(hop).start()
        return carry

    def finish(hop, carry):
        copy_to(hop).wait_send()
        copy_from(hop).wait_recv()
        return carry

    lax.fori_loop(1, devices, start, 0)
    in_ref[me] = out_ref[me]
    lax.fori_loop(1, devices, finish, 0)


def in_smem():
    return pl.BlockSpec(memory_space=pltpu.SMEM)


def in_vmem():
    return pl.BlockSpec(memory_space=pltpu.VMEM)


def outgoing_rows(send_rows, rows):
    node_rows, width = rows.shape
    parts = width // 128
    peers, slots = send_rows.shape
    return pl.pallas_call(
        outgoing_kernel,
        out_shape=jax.ShapeDtypeStruct((peers * slots, width), rows.dtype),
        in_specs=[in_smem(), in_vmem()],
        out_specs=in_vmem(),
        scratch_shapes=[
            pltpu.VMEM((node_rows * parts, 128), jnp.float32),
            pltpu.VMEM((slots * parts, 128), jnp.float32),
            pltpu.VMEM((slots * parts, 128), jnp.float32),
        ],
        compiler_params=pltpu.CompilerParams(vmem_limit_bytes=16 * 1024 * 1024),
        name="outgoing",
    )(send_rows, rows)


def pooled_means(name, edges, rows, incoming, relations):
    sources, windows, count, local_slot = edges
    node_rows, width = rows.shape
    parts = width // 128
    block_width = local_slot.shape[1]
    tiles = node_rows // WIN
    slots = WIN * relations
    table_rows = node_rows + incoming.shape[0]
    return pl.pallas_call(
        pool_kernel,
        out_shape=jax.ShapeDtypeStruct((relations, node_rows, width), jnp.bfloat16),
        in_specs=[in_smem()] * 3 + [in_vmem()] * 3,
        out_specs=in_vmem(),
        scratch_shapes=[
            pltpu.VMEM((table_rows * parts, 128), jnp.float32),
            pltpu.VMEM((block_width * parts, 128), jnp.float32),
            pltpu.VMEM((block_width * parts, 128), jnp.float32),
            pltpu.VMEM((tiles, slots, width), jnp.float32),
            pltpu.VMEM((tiles, slots, 128), jnp.float32),
        ],
        compiler_params=pltpu.CompilerParams(vmem_limit_bytes=VMEM_LIMIT),
        cost_estimate=pl.CostEstimate(
            flops=20_000_000_000, bytes_accessed=4_000_000, transcendentals=0
        ),
        name=name,
    )(sources, windows, count, local_slot, rows, incoming)


def dense_rows(name, send_rows, rows, means, weights, bias):
    node_rows, width = rows.shape
    parts = width // 128
    last = send_rows is None
    result = jax.ShapeDtypeStruct((node_rows, width), rows.dtype)
    scratch = []
    if not last:
        peers, slots = send_rows.shape
        scratch = [
            pltpu.VMEM((node_rows * parts, 128), jnp.float32),
            pltpu.VMEM((slots * parts, 128), jnp.float32),
            pltpu.VMEM((slots * parts, 128), jnp.float32),
        ]
    return pl.pallas_call(
        functools.partial(dense_kernel, last),
        out_shape=result
        if last
        else (result, jax.ShapeDtypeStruct((peers * slots, width), rows.dtype)),
        in_specs=[in_smem()] * (not last) + [in_vmem()] * 4,
        out_specs=in_vmem() if last else (in_vmem(), in_vmem()),
        scratch_shapes=scratch,
        compiler_params=pltpu.CompilerParams(vmem_limit_bytes=24 * 1024 * 1024),
        cost_estimate=pl.CostEstimate(
            flops=3_000_000_000, bytes_accessed=6_000_000, transcendentals=0
        ),
        name=name,
    )(*([] if last else [send_rows]), rows, means, weights, bias[None])


def exchange(outgoing, peers):
    slots = outgoing.shape[0] // peers
    shaped = outgoing.reshape(peers, slots, outgoing.shape[1])
    incoming = pl.pallas_call(
        functools.partial(exchange_kernel, peers),
        out_shape=jax.ShapeDtypeStruct(shaped.shape, shaped.dtype),
        in_specs=[in_vmem()],
        out_specs=in_vmem(),
        scratch_shapes=[
            pltpu.SemaphoreType.DMA((peers,)),
            pltpu.SemaphoreType.DMA((peers,)),
        ],
        compiler_params=pltpu.CompilerParams(
            has_side_effects=True, vmem_limit_bytes=16 * 1024 * 1024
        ),
        cost_estimate=pl.CostEstimate(
            flops=10_000_000_000, bytes_accessed=1_000_000, transcendentals=0
        ),
        name="exchange",
    )(shaped)
    return incoming.reshape(outgoing.shape)


def shards(
    features,
    edge_source,
    edge_relation,
    edge_target,
    block_count,
    send_list,
    bases_first,
    self_first,
    coef_first,
    bias_first,
    bases_second,
    self_second,
    coef_second,
    bias_second,
):
    targets = edge_target[0]
    windows = targets[:, 0] // WIN
    local_slot = edge_relation[0] * WIN + targets % WIN
    lanes = features.shape[1] // 128
    edges = (edge_source[0] * lanes, windows, block_count, local_slot)
    send_rows = send_list[0] * lanes
    peers = send_rows.shape[0]
    relations = coef_first.shape[0]
    width = features.shape[1]
    digits = digits_of(peers)
    share_first = weight_share(bases_first, self_first, coef_first)
    share_second = weight_share(bases_second, self_second, coef_second)

    along_x, along_y, along_z = digits

    early = jnp.concatenate([share_first, share_second], axis=0)
    early = gather_digit(early, peers, *along_x)
    share_first, share_second = early[: relations + 1], early[relations + 1 :]
    share_first = gather_digit(share_first, peers, *along_y)
    outgoing = outgoing_rows(send_rows, features)
    outgoing, share_first, share_second = lax.optimization_barrier(
        (outgoing, share_first, share_second)
    )
    incoming = exchange(outgoing, peers)
    incoming, share_first, share_second = lax.optimization_barrier(
        (incoming, share_first, share_second)
    )
    came_second = send_digit(share_second, peers, *along_y)
    came_first = send_digit(share_first, peers, *along_z)
    means = pooled_means("pool_first", edges, features, incoming, relations)
    means, came_first, came_second = lax.optimization_barrier((means, came_first, came_second))
    share_first = gather_digit(join_digit(share_first, came_first, *along_z), peers, 2, 1, True)
    share_second = join_digit(share_second, came_second, *along_y)
    weights_first = share_first.reshape(relations + 1, width, width)
    hidden, outgoing = dense_rows(
        "dense_first", send_rows, features, means, weights_first, bias_first
    )
    incoming = exchange(outgoing, peers)
    incoming, share_second = lax.optimization_barrier((incoming, share_second))
    came_second = send_digit(share_second, peers, *along_z)
    means = pooled_means("pool_second", edges, hidden, incoming, relations)
    means, came_second = lax.optimization_barrier((means, came_second))
    share_second = gather_digit(
        join_digit(share_second, came_second, *along_z), peers, 2, 1, True
    )
    weights_second = share_second.reshape(relations + 1, width, width)
    return dense_rows("dense_second", None, hidden, means, weights_second, bias_second)


def solution(mesh):
    placed = (
        P("dom", None),
        P("dom", None, None),
        P("dom", None, None),
        P("dom", None, None),
        P("dom"),
        P("dom", None, None),
        P(None, "dom", None),
        P("dom", None),
        P(),
        P(),
        P(None, "dom", None),
        P("dom", None),
        P(),
        P(),
    )
    return jax.shard_map(
        shards, mesh=mesh, in_specs=placed, out_specs=P("dom", None), check_vma=False
    )
```

profile of v0, /device:TPU:15, one launch (start us, length us, event | category | flops | bytes accessed | tf_op | source)
XLA Modules:
  0.0 132.2 jit_solution(2569811317506981993)
XLA Ops:
  0.0 0.8 copy.29
  0.8 0.7 copy.31
  1.5 0.9 convolution_convert_fusion.1
  2.3 1.1 convolution_convert_fusion
  3.8 0.9 slice_reduce_fusion
  4.8 0.7 multiply_bitcast_fusion.1.send_ref.refs_0_
  5.5 0.8 multiply_bitcast_fusion.source_ref
  6.3 0.9 fusion.6.slot_ref
  8.0 1.9 %outgoing.1 = bf16[1024,256]{1,0:T(8,128)(2,1)S(1)} custom-call(s32[32,32]{1,0:T(8,128)S(1)} %multiply_bitcast_fusion.1.send_ref.refs_0_, bf16[1024,256]{1,0:T(8,128)(2,1)S(1)} %copy-done.1), custom_call_target="tpu_custom_call" | custom-call | tf_op jit(solution)/shard_map/outgoing/pallas_call | solution.py:297
  10.4 3.5 %collective-permute-done.1 = bf16[9,2,8,256]{3,0,2,1:T(8,128)(2,1)S(1)} collective-permute-done((bf16[9,2,8,256]{3,0,2,1:T(8,128)(2,1)S(1)}, bf16[9,2,8,256]{3,0,2,1:T(8,128)(2,1)S(1)}, u32[]{:S(2)}, u32[]{:S(2)}) %collective-permute-start.1) | collective-permute-done | bytes 73760 | tf_op jit(solution)/shard_map/ppermute | solution.py:48
  14.0 21.9 %exchange.2 = bf16[32,32,256]{2,1,0:T(8,128)(2,1)S(1)} custom-call(bf16[32,32,256]{2,1,0:T(8,128)(2,1)S(1)} %bitcast.72), custom_call_target="tpu_custom_call" | custom-call | flops 10000000000 | bytes 1000000 | tf_op jit(solution)/shard_map/exchange/pallas_call | solution.py:372
  36.0 1.2 collective-permute-start.3
  37.2 2.3 %collective-permute-start.2 = (bf16[9,4,8,256]{3,0,2,1:T(8,128)(2,1)S(1)}, bf16[9,4,8,256]{3,0,2,1:T(8,128)(2,1)S(1)}, u32[]{:S(2)}, u32[]{:S(2)}) collective-permute-start(bf16[9,4,8,256]{3,0,2,1:T(8,128)(2,1)S(1)} %bitcast.88), channel_id=1, source_target_pairs={{0,8},{1,9},{2,10},{3,11},{4,12},{5,13},{6,14},{7,15},{8,16},{9,17... | collective-permute-start | bytes 442376 | tf_op jit(solution)/shard_map/ppermute | solution.py:48
  39.6 26.6 %pool_first.1.refs_2_ = bf16[8,1024,256]{2,1,0:T(8,128)(2,1)S(1)} custom-call(s32[128,128]{1,0:T(8,128)S(1)} %multiply_bitcast_fusion.source_ref, s32[128]{0:T(128)S(1)} %and_select_fusion.window_ref, s32[1]{0:T(128)S(6)} %copy.59.count_ref, s32[128,128]{1,0:T(8,128)S(1)} %fusion.6.slot_ref, bf16[1024,256]{1,0:T(8,128)(2,1)S(1)} %copy-done.1, ...), custom_call_target="tpu_custom_call" | custom-call | flops 20000000000 | bytes 4000000 | tf_op jit(solution)/shard_map/pool_first/pallas_call | solution.py:320
  66.2 1.9 %copy-done.4 = bf16[8,1024,256]{2,1,0:T(8,128)(2,1)} copy-done((bf16[8,1024,256]{2,1,0:T(8,128)(2,1)}, bf16[8,1024,256]{2,1,0:T(8,128)(2,1)S(1)}, u32[]{:S(2)}) %copy-start.4) | copy-done | bytes 4194328
  68.7 1.9 %collective-permute-done.6 = bf16[9,16,8,256]{3,2,1,0:T(8,128)(2,1)S(1)} collective-permute-done((bf16[9,16,8,256]{3,2,1,0:T(8,128)(2,1)S(1)}, bf16[9,16,8,256]{3,2,1,0:T(8,128)(2,1)S(1)}, u32[]{:S(2)}, u32[]{:S(2)}) %collective-permute-start.6) | collective-permute-done | bytes 589856 | tf_op jit(solution)/shard_map/ppermute | solution.py:48
  70.9 1.9 %copy-done.5 = bf16[8,1024,256]{2,1,0:T(8,128)(2,1)S(1)} copy-done((bf16[8,1024,256]{2,1,0:T(8,128)(2,1)S(1)}, bf16[8,1024,256]{2,1,0:T(8,128)(2,1)}, u32[]{:S(2)}) %copy-start.5) | copy-done | bytes 4194328
  72.9 3.7 %dense_first.1 = (bf16[1024,256]{1,0:T(8,128)(2,1)S(1)}, bf16[1024,256]{1,0:T(8,128)(2,1)S(1)}) custom-call(s32[32,32]{1,0:T(8,128)S(1)} %multiply_bitcast_fusion.1.send_ref.refs_0_, bf16[1024,256]{1,0:T(8,128)(2,1)S(1)} %copy-done.1, bf16[8,1024,256]{2,1,0:T(8,128)(2,1)S(1)} %copy-done.5, bf16[9,256,256]{2,1,0:T(8,128)(2,1)S(1)} %bitcast.70, ...), custom_call_target="tpu_custom_call" | custom-call | flops 3000000000 | bytes 6000000 | tf_op jit(solution)/shard_map/dense_first/pallas_call | solution.py:353
  76.6 19.4 %exchange.3 = bf16[32,32,256]{2,1,0:T(8,128)(2,1)S(1)} custom-call(bf16[32,32,256]{2,1,0:T(8,128)(2,1)S(1)} %bitcast.77), custom_call_target="tpu_custom_call" | custom-call | flops 10000000000 | bytes 1000000 | tf_op jit(solution)/shard_map/exchange/pallas_call | solution.py:372
  96.1 1.2 collective-permute-start.8
  97.3 2.3 %collective-permute-start.7 = (bf16[9,4,8,256]{3,0,2,1:T(8,128)(2,1)S(1)}, bf16[9,4,8,256]{3,0,2,1:T(8,128)(2,1)S(1)}, u32[]{:S(2)}, u32[]{:S(2)}) collective-permute-start(bf16[9,4,8,256]{3,0,2,1:T(8,128)(2,1)S(1)} %bitcast.84), channel_id=1, source_target_pairs={{0,8},{1,9},{2,10},{3,11},{4,12},{5,13},{6,14},{7,15},{8,16},{9,17... | collective-permute-start | bytes 442376 | tf_op jit(solution)/shard_map/ppermute | solution.py:48
  99.6 26.6 %pool_second.1.refs_1_ = bf16[8,1024,256]{2,1,0:T(8,128)(2,1)S(1)} custom-call(s32[128,128]{1,0:T(8,128)S(1)} %multiply_bitcast_fusion.source_ref, s32[128]{0:T(128)S(1)} %and_select_fusion.window_ref, s32[1]{0:T(128)S(6)} %copy.59.count_ref, s32[128,128]{1,0:T(8,128)S(1)} %fusion.6.slot_ref, bf16[1024,256]{1,0:T(8,128)(2,1)S(1)} %get-tuple-element.34.own_ref.refs_0_, ...), custom_call_target="tpu_custom_call" | custom-call | flops 20000000000 | bytes 4000000 | tf_op jit(solution)/shard_map/pool_second/pallas_call | solution.py:320
  126.7 2.0 %collective-permute-done.10 = bf16[9,16,8,256]{3,2,1,0:T(8,128)(2,1)S(1)} collective-permute-done((bf16[9,16,8,256]{3,2,1,0:T(8,128)(2,1)S(1)}, bf16[9,16,8,256]{3,2,1,0:T(8,128)(2,1)S(1)}, u32[]{:S(2)}, u32[]{:S(2)}) %collective-permute-start.10) | collective-permute-done | bytes 589856 | tf_op jit(solution)/shard_map/ppermute | solution.py:48
  129.5 2.7 %dense_second.1 = bf16[1024,256]{1,0:T(8,128)(2,1)} custom-call(bf16[1024,256]{1,0:T(8,128)(2,1)S(1)} %get-tuple-element.34.own_ref.refs_0_, bf16[8,1024,256]{2,1,0:T(8,128)(2,1)S(1)} %pool_second.1.refs_1_, bf16[9,256,256]{2,1,0:T(8,128)(2,1)S(1)} %bitcast.71, f32[1,256]{1,0:T(1,128)S(1)} %bitcast.74), custom_call_target="tpu_custom_call" | custom-call | flops 3000000000 | bytes 6000000 | tf_op jit(solution)/shard_map/dense_second/pallas_call | solution.py:353
  (51 shorter events, 3.0 us)
Async XLA Ops:
  0.0 1.5 %copy-start = (bf16[30,8,256]{2,1,0:T(8,128)(2,1)S(1)}, bf16[30,8,256]{2,1,0:T(8,128)(2,1)}, u32[]{:S(2)}) copy-start(bf16[30,8,256]{2,1,0:T(8,128)(2,1)} %param.20) | copy-start | bytes 368644
  0.0 8.0 %copy-start.1 = (bf16[1024,256]{1,0:T(8,128)(2,1)S(1)}, bf16[1024,256]{1,0:T(8,128)(2,1)}, u32[]{:S(2)}) copy-start(bf16[1024,256]{1,0:T(8,128)(2,1)} %refs_1_.1) | copy-start | bytes 1572868
  3.5 6.4 %collective-permute-start = (bf16[18,1,8,256]{3,0,2,1:T(8,128)(2,1)S(1)}, bf16[18,1,8,256]{3,0,2,1:T(8,128)(2,1)S(1)}, u32[]{:S(2)}, u32[]{:S(2)}) collective-permute-start(bf16[18,1,8,256]{3,0,2,1:T(8,128)(2,1)S(1)} %pad_maximum_fusion.5), channel_id=1, source_target_pairs={{0,2},{1,3},{2,0},{3,1},{4,6},{5,7},{6,4},{7,5},{8,10},{9,11},{10,... | collective-permute-start | bytes 221192 | tf_op jit(solution)/shard_map/ppermute | solution.py:48
  10.0 3.9 %collective-permute-start.1 = (bf16[9,2,8,256]{3,0,2,1:T(8,128)(2,1)S(1)}, bf16[9,2,8,256]{3,0,2,1:T(8,128)(2,1)S(1)}, u32[]{:S(2)}, u32[]{:S(2)}) collective-permute-start(bf16[9,2,8,256]{3,0,2,1:T(8,128)(2,1)S(1)} %slice_bitcast_fusion), channel_id=1, source_target_pairs={{0,4},{1,5},{2,6},{3,7},{4,0},{5,1},{6,2},{7,3},{8,12},{9,13},{10,... | collective-permute-start | bytes 221192 | tf_op jit(solution)/shard_map/ppermute | solution.py:48
  35.9 32.3 %collective-permute-start.4 = (bf16[9,4,8,256]{3,0,2,1:T(8,128)(2,1)S(1)}, bf16[9,4,8,256]{3,0,2,1:T(8,128)(2,1)S(1)}, u32[]{:S(2)}, u32[]{:S(2)}) collective-permute-start(bf16[9,4,8,256]{3,0,2,1:T(8,128)(2,1)S(1)} %bitcast.86), channel_id=1, source_target_pairs={{0,24},{1,25},{2,26},{3,27},{4,28},{5,29},{6,30},{7,31},{8,0},{9,1... | collective-permute-start | bytes 442376 | tf_op jit(solution)/shard_map/ppermute | solution.py:48
  36.0 32.2 %collective-permute-start.3 = (bf16[9,4,8,256]{3,0,2,1:T(8,128)(2,1)S(1)}, bf16[9,4,8,256]{3,0,2,1:T(8,128)(2,1)S(1)}, u32[]{:S(2)}, u32[]{:S(2)}) collective-permute-start(bf16[9,4,8,256]{3,0,2,1:T(8,128)(2,1)S(1)} %bitcast.87), channel_id=1, source_target_pairs={{0,16},{1,17},{2,18},{3,19},{4,20},{5,21},{6,22},{7,23},{8,24},{9,... | collective-permute-start | bytes 442376 | tf_op jit(solution)/shard_map/ppermute | solution.py:48
  37.2 31.0 %collective-permute-start.2 = (bf16[9,4,8,256]{3,0,2,1:T(8,128)(2,1)S(1)}, bf16[9,4,8,256]{3,0,2,1:T(8,128)(2,1)S(1)}, u32[]{:S(2)}, u32[]{:S(2)}) collective-permute-start(bf16[9,4,8,256]{3,0,2,1:T(8,128)(2,1)S(1)} %bitcast.88), channel_id=1, source_target_pairs={{0,8},{1,9},{2,10},{3,11},{4,12},{5,13},{6,14},{7,15},{8,16},{9,17... | collective-permute-start | bytes 442376 | tf_op jit(solution)/shard_map/ppermute | solution.py:48
  39.5 28.7 %collective-permute-start.5 = (bf16[9,2,8,256]{3,0,2,1:T(8,128)(2,1)S(1)}, bf16[9,2,8,256]{3,0,2,1:T(8,128)(2,1)S(1)}, u32[]{:S(2)}, u32[]{:S(2)}) collective-permute-start(bf16[9,2,8,256]{3,0,2,1:T(8,128)(2,1)S(1)} %fusion.2), channel_id=1, source_target_pairs={{0,4},{1,5},{2,6},{3,7},{4,0},{5,1},{6,2},{7,3},{8,12},{9,13},{10,... | collective-permute-start | bytes 221192 | tf_op jit(solution)/shard_map/ppermute | solution.py:48
  66.2 1.9 %copy-start.4 = (bf16[8,1024,256]{2,1,0:T(8,128)(2,1)}, bf16[8,1024,256]{2,1,0:T(8,128)(2,1)S(1)}, u32[]{:S(2)}) copy-start(bf16[8,1024,256]{2,1,0:T(8,128)(2,1)S(1)} %pool_first.1.refs_2_) | copy-start | bytes 12582916
  68.5 2.1 %collective-permute-start.6 = (bf16[9,16,8,256]{3,2,1,0:T(8,128)(2,1)S(1)}, bf16[9,16,8,256]{3,2,1,0:T(8,128)(2,1)S(1)}, u32[]{:S(2)}, u32[]{:S(2)}) collective-permute-start(bf16[9,16,8,256]{3,2,1,0:T(8,128)(2,1)S(1)} %bitcast.80), channel_id=1, source_target_pairs={{0,1},{1,0},{2,3},{3,2},{4,5},{5,4},{6,7},{7,6},{8,9},{9,8},{10,11... | collective-permute-start | bytes 1769480 | tf_op jit(solution)/shard_map/ppermute | solution.py:48
  70.7 2.2 %copy-start.5 = (bf16[8,1024,256]{2,1,0:T(8,128)(2,1)S(1)}, bf16[8,1024,256]{2,1,0:T(8,128)(2,1)}, u32[]{:S(2)}) copy-start(bf16[8,1024,256]{2,1,0:T(8,128)(2,1)} %copy-done.4) | copy-start | bytes 12582916
  70.8 2.1 %copy-start.2 = (f32[256]{0:T(256)S(1)}, f32[256]{0:T(256)}, u32[]{:S(2)}) copy-start(f32[256]{0:T(256)} %param.23) | copy-start | bytes 3076
  96.0 30.3 %collective-permute-start.9 = (bf16[9,4,8,256]{3,0,2,1:T(8,128)(2,1)S(1)}, bf16[9,4,8,256]{3,0,2,1:T(8,128)(2,1)S(1)}, u32[]{:S(2)}, u32[]{:S(2)}) collective-permute-start(bf16[9,4,8,256]{3,0,2,1:T(8,128)(2,1)S(1)} %bitcast.82), channel_id=1, source_target_pairs={{0,24},{1,25},{2,26},{3,27},{4,28},{5,29},{6,30},{7,31},{8,0},{9,1... | collective-permute-start | bytes 442376 | tf_op jit(solution)/shard_map/ppermute | solution.py:48
  96.1 30.2 %collective-permute-start.8 = (bf16[9,4,8,256]{3,0,2,1:T(8,128)(2,1)S(1)}, bf16[9,4,8,256]{3,0,2,1:T(8,128)(2,1)S(1)}, u32[]{:S(2)}, u32[]{:S(2)}) collective-permute-start(bf16[9,4,8,256]{3,0,2,1:T(8,128)(2,1)S(1)} %bitcast.83), channel_id=1, source_target_pairs={{0,16},{1,17},{2,18},{3,19},{4,20},{5,21},{6,22},{7,23},{8,24},{9,... | collective-permute-start | bytes 442376 | tf_op jit(solution)/shard_map/ppermute | solution.py:48
  97.3 29.0 %collective-permute-start.7 = (bf16[9,4,8,256]{3,0,2,1:T(8,128)(2,1)S(1)}, bf16[9,4,8,256]{3,0,2,1:T(8,128)(2,1)S(1)}, u32[]{:S(2)}, u32[]{:S(2)}) collective-permute-start(bf16[9,4,8,256]{3,0,2,1:T(8,128)(2,1)S(1)} %bitcast.84), channel_id=1, source_target_pairs={{0,8},{1,9},{2,10},{3,11},{4,12},{5,13},{6,14},{7,15},{8,16},{9,17... | collective-permute-start | bytes 442376 | tf_op jit(solution)/shard_map/ppermute | solution.py:48
  126.6 2.1 %collective-permute-start.10 = (bf16[9,16,8,256]{3,2,1,0:T(8,128)(2,1)S(1)}, bf16[9,16,8,256]{3,2,1,0:T(8,128)(2,1)S(1)}, u32[]{:S(2)}, u32[]{:S(2)}) collective-permute-start(bf16[9,16,8,256]{3,2,1,0:T(8,128)(2,1)S(1)} %bitcast.78), channel_id=1, source_target_pairs={{0,1},{1,0},{2,3},{3,2},{4,5},{5,4},{6,7},{7,6},{8,9},{9,8},{10,11... | collective-permute-start | bytes 1769480 | tf_op jit(solution)/shard_map/ppermute | solution.py:48
  128.8 0.7 copy-start.3
where the time goes:
time: 133 us; the launch traced here: 132 us
  Pallas kernels  103 us (77%)
  starting transfers between devices  7.96 us (6%)
  local copies, waits for them, and re-layouts  7.53 us (6%)
  waiting for transfers between devices  7.46 us (6%)
  other arithmetic  3.23 us (2%)
  matrix products  1.95 us (1%)
    pallas_call x2, Pallas kernels, pooled_means(): pl.pallas_call(pool_kernel, out_shape=jax.ShapeDtypeStruct((relations, no...  53.2 us
    pallas_call x2, Pallas kernels, exchange(): pl.pallas_call(functools.partial(exchange_kernel, peers), out_shape=jax.S...  41.4 us
    ppermute x11, starting transfers between devices, send_digit(): lax.ppermute(share, 'dom', shift_pairs(devices, radix, stride, hop))  7.96 us
    ppermute x11, waiting for transfers between devices, send_digit(): lax.ppermute(share, 'dom', shift_pairs(devices, radix, stride, hop))  7.46 us
    pallas_call x2, Pallas kernels, dense_rows(): pl.pallas_call(functools.partial(dense_kernel, last), out_shape=result if...  6.44 us
    unnamed x12, local copies, waits for them, and re-layouts  4.46 us
  transfers between devices with their start and end apart: 11, of which 3 were waited for; matrix products, arithmetic and copies ran while one was open for 3% of the time, Pallas kernels for 42%

commit v1 on v0

v1 whole, which is shorter than its diff:
```python
import functools
import math

import jax
import jax.numpy as jnp
from jax import lax
from jax.experimental import pallas as pl
from jax.experimental.pallas import tpu as pltpu
from jax.sharding import PartitionSpec as P

WIN = 16
OWN, NEAR, FAR, COUNT, SPREAD = 16, 16, 16, 32, 16
VMEM_LIMIT = 63 * 1024 * 1024
MESH = pl.DeviceIdType.MESH


def sides(devices):
    chips = devices // 2
    side = max(math.isqrt(chips // 4), 1)
    return chips // (side * side), side, side, 2


def one_hot(columns, first, count):
    lanes = lax.broadcasted_iota(jnp.int32, columns.shape, 1)
    parts = [
        (columns == lanes + (first + part * 128)).astype(jnp.float32).astype(jnp.bfloat16)
        for part in range(count // 128)
    ]
    return jnp.concatenate(parts, axis=1)


def fused_kernel(
    devices,
    source_ref,
    relation_ref,
    target_ref,
    send_ref,
    count_ref,
    features_ref,
    bases_a,
    self_a,
    bases_b,
    self_b,
    coef_a,
    coef_b,
    bias_a,
    bias_b,
    out_ref,
    column_ref,
    picked_ref,
    pooled_ref,
    inverse_ref,
    mean_ref,
    weight_ref,
    pieces_a,
    pieces_b,
    slot_ref,
    send_column_ref,
    sent,
    came_a,
    came_b,
    hidden_ref,
    plan_ref,
    plan_smem,
    plan_sem,
    send_sems,
    recv_sems,
    piece_send_sems,
    piece_recv_sems,
):
    me = lax.axis_index("dom")
    planes, rows_y, rows_x, cores = sides(devices)
    low = rows_y * rows_x * cores
    my_z, my_low = me // low, me % low
    my_y = my_low // (rows_x * cores)
    my_x = my_low // cores % rows_x
    my_core = my_low % cores
    node_rows, width = features_ref.shape
    blocks, edges = source_ref.shape
    peers, slots = send_ref.shape
    relations, bases = coef_a.shape
    share = self_a.shape[0]
    windows = node_rows // WIN
    places = WIN * relations
    plane_rows = low * slots

    def at(z, y, x, core):
        return ((z * rows_y + y) * rows_x + x) * cores + core

    barrier = pltpu.get_barrier_semaphore()

    def greet(hop, carry):
        peer = lax.rem(me + hop, devices)
        pl.semaphore_signal(barrier, inc=1, device_id=(peer,), device_id_type=MESH)
        return carry

    lax.fori_loop(1, devices, greet, 0)

    def compose(bases_ref, self_ref, coef_ref, pieces):
        sums = [jnp.zeros((share, width), jnp.float32) for _ in range(relations)]
        for basis in range(bases):
            matrix = bases_ref[basis].astype(jnp.float32)
            sums = [
                total + coef_ref[relation, basis] * matrix for relation, total in enumerate(sums)
            ]
        for relation, total in enumerate(sums):
            pieces[my_z, my_y, my_x, my_core, relation] = total.astype(jnp.bfloat16)
        pieces[my_z, my_y, my_x, my_core, relations] = self_ref[...]

    compose(bases_a, self_a, coef_a, pieces_a)
    compose(bases_b, self_b, coef_b, pieces_b)

    lane_ids = lax.broadcasted_iota(jnp.int32, (edges, 128), 1)
    row_ids = lax.broadcasted_iota(jnp.int32, (edges, 128), 0)
    eye = row_ids == lane_ids
    eye_send = lax.broadcasted_iota(jnp.int32, (slots, slots), 0) == lax.broadcasted_iota(
        jnp.int32, (slots, slots), 1
    )

    def send_columns(group, carry):
        listed = send_ref[pl.ds(pl.multiple_of(group * 8, 8), 8), :]
        for row in range(8):
            spread = jnp.where(eye_send, listed[row : row + 1, :], 0).astype(jnp.float32)
            column = jnp.sum(spread, axis=1, keepdims=True)
            first = pl.multiple_of((group * 8 + row) * slots, slots)
            send_column_ref[pl.ds(first, slots), :] = jnp.broadcast_to(
                column, (slots, 128)
            ).astype(jnp.int32)
        return carry

    lax.fori_loop(0, peers // 8, send_columns, 0)

    def plan():
        window_c = jnp.broadcast_to(target_ref[:, 0:1] // WIN, (blocks, 128))
        window_r = jnp.sum(jnp.where(eye, window_c, 0), axis=0, keepdims=True)
        key_c = window_c * blocks + row_ids
        key_r = window_r * blocks + lane_ids[0:1]
        before = jnp.where(key_c < key_r, 1, 0)
        rank_r = jnp.sum(before, axis=0, keepdims=True)
        same = jnp.where(window_c == window_r, before, 0)
        follows_r = jnp.minimum(jnp.sum(same, axis=0, keepdims=True), 1)
        rank_c = jnp.transpose(jnp.broadcast_to(rank_r, (128, 128)))
        follows_c = jnp.transpose(jnp.broadcast_to(follows_r, (128, 128)))
        placed = rank_c == lane_ids
        order = jnp.sum(jnp.where(placed, row_ids, 0), axis=0, keepdims=True)
        keep = jnp.sum(jnp.where(placed, follows_c, 0), axis=0, keepdims=True)
        last = jnp.max(
            jnp.where(window_c == lane_ids, rank_c + 1, 0), axis=0, keepdims=True
        )
        plan_ref[...] = jnp.concatenate(
            [order, keep, last, jnp.zeros((5, 128), jnp.int32)], axis=0
        )

    plan()

    slot = relation_ref[...] * WIN + target_ref[...] % WIN
    slot_ref[...] = jnp.where(row_ids < count_ref[0], slot, -1).reshape(blocks, 1, edges)

    def copies(layer, stage):
        pieces = (pieces_a, pieces_b)[layer]
        made = []
        if stage == 0:
            count, source = planes, lambda: pieces.at[my_z, my_y, my_x, my_core]
        elif stage == 1:
            count, source = rows_y, lambda: pieces.at[:, my_y, my_x, my_core]
        elif stage == 2:
            count, source = rows_x, lambda: pieces.at[:, :, my_x, my_core]
        else:
            count, source = cores, lambda: pieces.at[:, :, :, my_core]
        for hop in range(1, count):
            to = [my_z, my_y, my_x, my_core]
            to[stage] = lax.rem(to[stage] + hop, count)
            by = [my_z, my_y, my_x, my_core]
            by[stage] = lax.rem(by[stage] + count - hop, count)
            landed = pieces.at[(*(slice(None),) * stage, by[stage], *by[stage + 1 :])]
            if stage == 0:
                landed = pieces.at[by[0], my_y, my_x, my_core]
            pair = (layer, stage, hop)
            sems = dict(
                send_sem=piece_send_sems.at[pair],
                recv_sem=piece_recv_sems.at[pair],
                device_id=(at(*to),),
                device_id_type=MESH,
            )
            made.append(
                (
                    pltpu.make_async_remote_copy(src_ref=source(), dst_ref=source(), **sems),
                    pltpu.make_async_remote_copy(src_ref=landed, dst_ref=landed, **sems),
                )
            )
        return made

    def send_pieces(layer, stage):
        for out, _ in copies(layer, stage):
            out.start()

    def land_pieces(layer, stage):
        for out, landed in copies(layer, stage):
            out.wait_send()
            landed.wait_recv()

    def join_pieces(layer):
        pieces = (pieces_a, pieces_b)[layer]

        group = max(16 // share, 1)
        height = group * share

        def join(step, carry):
            for relation in range(relations + 1):
                rows = []
                for part in range(group):
                    device = step * group + part
                    z, rest = device // low, device % low
                    y, rest = rest // (rows_x * cores), rest % (rows_x * cores)
                    rows.append(
                        pieces[z, y, rest // cores, rest % cores, relation].astype(jnp.float32)
                    )
                first = pl.multiple_of(step * height, height)
                weight_ref[relation, pl.ds(first, height), :] = (
                    rows[0] if group == 1 else jnp.concatenate(rows, axis=0)
                ).astype(jnp.bfloat16)
            return carry

        lax.fori_loop(0, devices // group, join, 0)

    def peer_of(hop_z, hop_low, sign):
        z = lax.rem(my_z + planes + sign * hop_z, planes)
        rest = lax.rem(my_low + low + sign * hop_low, low)
        return z * low + rest

    def row_copy(layer, hop_z, hop_low, landing):
        came = (came_a, came_b)[layer]
        hop = hop_z * low + hop_low
        to = peer_of(hop_z, hop_low, 1)
        owner = peer_of(hop_z, hop_low, -1) if landing else me
        return pltpu.make_async_remote_copy(
            src_ref=sent.at[pl.ds(pl.multiple_of(to * slots, slots), slots)],
            dst_ref=came.at[pl.ds(pl.multiple_of(owner * slots, slots), slots)],
            send_sem=send_sems.at[layer, hop],
            recv_sem=recv_sems.at[layer, hop],
            device_id=(to,),
            device_id_type=MESH,
        )

    def plane_order():
        return sorted(range(planes), key=lambda hop: -min(hop, planes - hop))

    def pick_plane(layer, rows_ref, hop_z):
        z = lax.rem(my_z + hop_z, planes)
        for part in range(plane_rows // 256):
            first = pl.multiple_of(z * plane_rows + part * 256, 256)
            hot = one_hot(send_column_ref[pl.ds(first, 256), :], 0, node_rows)
            sent[pl.ds(first, 256), :] = jnp.dot(
                hot, rows_ref[...], preferred_element_type=jnp.float32
            ).astype(jnp.bfloat16)

    def start_plane(layer, hop_z):
        def start(hop_low, carry):
            row_copy(layer, hop_z, hop_low, False).start()
            return carry

        lax.fori_loop(1 if hop_z == 0 else 0, low, start, 0)

    def land_plane(layer, hop_z):
        def land(hop_low, carry):
            row_copy(layer, hop_z, hop_low, False).wait_send()
            row_copy(layer, hop_z, hop_low, True).wait_recv()
            return carry

        lax.fori_loop(1 if hop_z == 0 else 0, low, land, 0)

    place_ids = lax.broadcasted_iota(jnp.int32, (places, edges), 0)

    def send_rows(layer, rows_ref):
        came = (came_a, came_b)[layer]
        came[pl.ds(pl.multiple_of(me * slots, slots), slots), :] = jnp.zeros(
            (slots, width), jnp.bfloat16
        )
        waiting = None
        for hop_z in plane_order():
            pick_plane(layer, rows_ref, hop_z)
            if waiting is not None:
                start_plane(layer, waiting)
            waiting = hop_z
        return waiting

    def own_stage(rows_ref):
        def pick(step, carry):
            part = pl.ds(step * OWN, OWN)
            hot = one_hot(column_ref[part].reshape(OWN * edges, 128), 0, node_rows)
            picked_ref[part] = (
                jnp.dot(hot, rows_ref[...], preferred_element_type=jnp.float32)
                .astype(jnp.bfloat16)
                .reshape(OWN, edges, width)
            )
            return carry

        lax.fori_loop(0, blocks // OWN, pick, 0)

    def plane_parts(layer, columns, hops):
        came = (came_a, came_b)[layer]
        total = None
        for hop_z in hops:
            z = lax.rem(my_z + planes - hop_z, planes)
            hot = one_hot(columns, node_rows + z * plane_rows, plane_rows)
            rows = came[pl.ds(pl.multiple_of(z * plane_rows, plane_rows), plane_rows), :]
            part = jnp.dot(hot, rows, preferred_element_type=jnp.float32)
            total = part if total is None else total + part
        return total.astype(jnp.bfloat16)

    def near_stage(layer, hops):
        def pick(step, carry):
            part = pl.ds(step * NEAR, NEAR)
            columns = column_ref[part].reshape(NEAR * edges, 128)
            picked_ref[part] += plane_parts(layer, columns, hops).reshape(NEAR, edges, width)
            return carry

        lax.fori_loop(0, blocks // NEAR, pick, 0)

    def block_at(step):
        return jnp.clip(plan_smem[0, step], 0, blocks - 1)

    def last_of(window):
        return jnp.clip(plan_smem[2, window], 0, blocks)

    def hot_of(block):
        return (place_ids == slot_ref[block]).astype(jnp.float32).astype(jnp.bfloat16)

    def far_stage(layer, hops):
        def pool(step, carry):
            named = [block_at(step * FAR + part) for part in range(FAR)]
            columns = jnp.concatenate([column_ref[block] for block in named], axis=0)
            gathered = plane_parts(layer, columns, hops)
            total = pooled_ref[step * FAR]
            for part in range(FAR):
                messages = (
                    gathered[part * edges : (part + 1) * edges] + picked_ref[named[part]]
                )
                sums = jnp.dot(
                    hot_of(named[part]), messages, preferred_element_type=jnp.float32
                )
                keep = plan_smem[1, step * FAR + part].astype(jnp.float32)
                total = total * keep + sums
                pooled_ref[step * FAR + part + 1] = total
            return carry

        lax.fori_loop(0, blocks // FAR, pool, 0)

    def degree_stage():
        ones = jnp.ones((edges, 128), jnp.bfloat16)

        def pool(step, carry):
            total = pooled_ref[step * COUNT, :, 0:128]
            for part in range(COUNT):
                block = block_at(step * COUNT + part)
                numbers = jnp.dot(hot_of(block), ones, preferred_element_type=jnp.float32)
                keep = plan_smem[1, step * COUNT + part].astype(jnp.float32)
                total = total * keep + numbers
                pooled_ref[step * COUNT + part + 1, :, 0:128] = total
            return carry

        lax.fori_loop(0, blocks // COUNT, pool, 0)

        def invert(window, carry):
            numbers = pooled_ref[last_of(window), :, 0:128]
            inverse_ref[window] = 1.0 / jnp.maximum(numbers, 1.0)
            return carry

        lax.fori_loop(0, windows, invert, 0)

    def mean_stage():
        def average(window, carry):
            block = last_of(window)
            first = pl.multiple_of(window * WIN, WIN)
            for relation in range(relations):
                part = slice(relation * WIN, (relation + 1) * WIN)
                inverse = inverse_ref[window, part, :]
                for lane in range(0, width, 128):
                    mean_ref[relation, pl.ds(first, WIN), lane : lane + 128] = (
                        pooled_ref[block, part, lane : lane + 128] * inverse
                    ).astype(jnp.bfloat16)
            return carry

        lax.fori_loop(0, windows, average, 0)

    def dense_stage(rows_ref, bias_ref, result_ref, last):
        def dense(chunk, carry):
            rows = pl.ds(pl.multiple_of(chunk * 256, 256), 256)
            total = bias_ref[...] + jnp.dot(
                rows_ref[rows, :], weight_ref[relations], preferred_element_type=jnp.float32
            )
            for relation in range(relations):
                total = total + jnp.dot(
                    mean_ref[relation, rows, :],
                    weight_ref[relation],
                    preferred_element_type=jnp.float32,
                )
            if not last:
                total = jnp.maximum(total, 0.0)
            result_ref[rows, :] = total.astype(jnp.bfloat16)
            return carry

        lax.fori_loop(0, node_rows // 256, dense, 0)

    def source_columns():
        turned = jnp.transpose(source_ref[...].astype(jnp.float32))

        def spread(group, carry):
            rolled = pltpu.roll(turned, blocks - group * SPREAD, 1)
            for row in range(SPREAD):
                column_ref[group * SPREAD + row] = jnp.broadcast_to(
                    rolled[:, row : row + 1], (edges, 128)
                ).astype(jnp.int32)
            return carry

        lax.fori_loop(0, blocks // SPREAD, spread, 0)

    near = [planes // 2, 0] if planes > 2 else list(range(planes))
    far = [hop for hop in range(planes) if hop not in near]

    scope = jax.named_scope
    plan_copy = pltpu.make_async_copy(plan_ref, plan_smem, plan_sem)
    with scope("columns"):
        source_columns()
    plan_copy.start()
    pooled_ref[0] = jnp.zeros(pooled_ref.shape[1:], jnp.float32)
    with scope("greeted"):
        pl.semaphore_wait(barrier, devices - 1)
    send_pieces(0, 0)
    with scope("send_a"):
        waiting = send_rows(0, features_ref)
    plan_copy.wait()
    start_plane(0, waiting)
    with scope("degree"):
        degree_stage()
    with scope("piece_z"):
        land_pieces(0, 0)
    send_pieces(0, 1)
    with scope("own_a"):
        own_stage(features_ref)
    with scope("piece_y"):
        land_pieces(0, 1)
    send_pieces(0, 2)
    with scope("land_near_a"):
        for hop in near:
            land_plane(0, hop)
    with scope("near_a"):
        near_stage(0, near)
    with scope("land_far_a"):
        for hop in far:
            land_plane(0, hop)
    with scope("piece_x"):
        land_pieces(0, 2)
    send_pieces(0, 3)
    send_pieces(1, 0)
    with scope("far_a"):
        far_stage(0, far)
    with scope("piece_z_b"):
        land_pieces(1, 0)
    send_pieces(1, 1)
    with scope("mean_a"):
        mean_stage()
    with scope("piece_core"):
        land_pieces(0, 3)
    with scope("join_a"):
        join_pieces(0)
    with scope("dense_a"):
        dense_stage(features_ref, bias_a, hidden_ref, False)

    with scope("piece_y_b"):
        land_pieces(1, 1)
    send_pieces(1, 2)
    with scope("send_b"):
        waiting = send_rows(1, hidden_ref)
    start_plane(1, waiting)
    with scope("own_b"):
        own_stage(hidden_ref)
    with scope("piece_x_b"):
        land_pieces(1, 2)
    send_pieces(1, 3)
    with scope("land_near_b"):
        for hop in near:
            land_plane(1, hop)
    with scope("near_b"):
        near_stage(1, near)
    with scope("piece_core_b"):
        land_pieces(1, 3)
    with scope("join_b"):
        join_pieces(1)
    with scope("land_far_b"):
        for hop in far:
            land_plane(1, hop)
    with scope("far_b"):
        far_stage(1, far)
    with scope("mean_b"):
        mean_stage()
    with scope("dense_b"):
        dense_stage(hidden_ref, bias_b, out_ref, True)


def in_smem():
    return pl.BlockSpec(memory_space=pltpu.SMEM)


def in_vmem():
    return pl.BlockSpec(memory_space=pltpu.VMEM)


def shards(
    devices,
    features,
    edge_source,
    edge_relation,
    edge_target,
    block_count,
    send_list,
    bases_first,
    self_first,
    coef_first,
    bias_first,
    bases_second,
    self_second,
    coef_second,
    bias_second,
):
    node_rows, width = features.shape
    _, blocks, edges = edge_source.shape
    _, peers, slots = send_list.shape
    relations = coef_first.shape[0]
    share = self_first.shape[0]
    planes, rows_y, rows_x, cores = sides(devices)
    windows = node_rows // WIN
    places = WIN * relations
    came = peers * slots
    bf16, f32, i32 = jnp.bfloat16, jnp.float32, jnp.int32
    piece = (planes, rows_y, rows_x, cores, relations + 1, share, width)
    most = max(planes, rows_y, rows_x, cores)
    return pl.pallas_call(
        functools.partial(fused_kernel, devices),
        out_shape=jax.ShapeDtypeStruct((node_rows, width), bf16),
        in_specs=[in_vmem()] * 4
        + [in_smem()]
        + [in_vmem()] * 5
        + [in_smem()] * 2
        + [in_vmem()] * 2,
        out_specs=in_vmem(),
        scratch_shapes=[
            pltpu.VMEM((blocks, edges, 128), i32),
            pltpu.VMEM((blocks, edges, width), bf16),
            pltpu.VMEM((blocks + 1, places, width), f32),
            pltpu.VMEM((windows, places, 128), f32),
            pltpu.VMEM((relations, node_rows, width), bf16),
            pltpu.VMEM((relations + 1, width, width), bf16),
            pltpu.VMEM(piece, bf16),
            pltpu.VMEM(piece, bf16),
            pltpu.VMEM((blocks, 1, edges), i32),
            pltpu.VMEM((came, 128), i32),
            pltpu.VMEM((came, width), bf16),
            pltpu.VMEM((came, width), bf16),
            pltpu.VMEM((came, width), bf16),
            pltpu.VMEM((node_rows, width), bf16),
            pltpu.VMEM((8, 128), i32),
            pltpu.SMEM((8, 128), i32),
            pltpu.SemaphoreType.DMA,
            pltpu.SemaphoreType.DMA((2, peers)),
            pltpu.SemaphoreType.DMA((2, peers)),
            pltpu.SemaphoreType.DMA((2, 4, most)),
            pltpu.SemaphoreType.DMA((2, 4, most)),
        ],
        compiler_params=pltpu.CompilerParams(
            collective_id=0, has_side_effects=True, vmem_limit_bytes=VMEM_LIMIT
        ),
        name="rgcn",
    )(
        edge_source[0],
        edge_relation[0],
        edge_target[0],
        send_list[0],
        block_count,
        features,
        bases_first,
        self_first,
        bases_second,
        self_second,
        coef_first,
        coef_second,
        bias_first[None],
        bias_second[None],
    )


def solution(mesh):
    placed = (
        P("dom", None),
        P("dom", None, None),
        P("dom", None, None),
        P("dom", None, None),
        P("dom"),
        P("dom", None, None),
        P(None, "dom", None),
        P("dom", None),
        P(),
        P(),
        P(None, "dom", None),
        P("dom", None),
        P(),
        P(),
    )
    return jax.shard_map(
        functools.partial(shards, mesh.shape["dom"]),
        mesh=mesh,
        in_specs=placed,
        out_specs=P("dom", None),
        check_vma=False,
    )
```

time: 133 us -> 85.8 us (0.65)
  the two profiles are of different devices: /device:TPU:15 before, /device:TPU:8 now
where the time goes in v1:
time: 85.8 us; the launch traced here: 85.6 us
  Pallas kernels  83.1 us (97%)
  local copies, waits for them, and re-layouts  1.87 us (2%)
    pallas_call x1, Pallas kernels, shards(): pl.pallas_call(functools.partial(fused_kernel, devices), out_shape=jax.Sh...  83.1 us
    unnamed x1, local copies, waits for them, and re-layouts  1.87 us

profile of v1, /device:TPU:8, one launch (start us, length us, event | category | flops | bytes accessed | tf_op | source)
XLA Modules:
  0.0 85.6 jit_solution(10644054323462608759)
XLA Ops:
  0.7 83.1 %rgcn.1 = bf16[1024,256]{1,0:T(8,128)(2,1)} custom-call(s32[128,128]{1,0:T(8,128)} %bitcast.6, s32[128,128]{1,0:T(8,128)} %bitcast.7, s32[128,128]{1,0:T(8,128)} %bitcast.8, s32[32,32]{1,0:T(8,128)} %bitcast.9, s32[1]{0:T(128)S(6)} %copy.16.count_ref, bf16[1024,256]{1,0:T(8,128)(2,1)} %features_ref.1, bf16[30,8,256]{2,1,0:T(8,128)(2,1)} %bases_a.1, ...), custom_call_target="tpu_custom_call" | custom-call | tf_op jit(solution)/shard_map/rgcn/pallas_call | solution.py:538
  83.7 1.9 %copy.17 = bf16[1024,256]{1,0:T(8,128)(2,1)} copy(bf16[1024,256]{1,0:T(8,128)(2,1)} %rgcn.1) | data formatting | bytes 1048576

commit v2 on v1

--- a/solution.py
+++ b/solution.py
@@ -9,7 +9,7 @@
 from jax.sharding import PartitionSpec as P
 
 WIN = 16
-OWN, NEAR, FAR, COUNT, SPREAD = 16, 16, 16, 32, 16
+POOL, COUNT, SPREAD = 16, 32, 16
 VMEM_LIMIT = 63 * 1024 * 1024
 MESH = pl.DeviceIdType.MESH
 
@@ -18,6 +18,13 @@
     chips = devices // 2
     side = max(math.isqrt(chips // 4), 1)
     return chips // (side * side), side, side, 2
+
+
+def group_of(depth):
+    group = 32
+    while group * depth > 32 * 1024:
+        group //= 2
+    return group
 
 
 def one_hot(columns, first, count):
@@ -108,7 +115,6 @@
         pieces[my_z, my_y, my_x, my_core, relations] = self_ref[...]
 
     compose(bases_a, self_a, coef_a, pieces_a)
-    compose(bases_b, self_b, coef_b, pieces_b)
 
     lane_ids = lax.broadcasted_iota(jnp.int32, (edges, 128), 1)
     row_ids = lax.broadcasted_iota(jnp.int32, (edges, 128), 0)
@@ -285,17 +291,19 @@
         return waiting
 
     def own_stage(rows_ref):
+        group = group_of(node_rows)
+
         def pick(step, carry):
-            part = pl.ds(step * OWN, OWN)
-            hot = one_hot(column_ref[part].reshape(OWN * edges, 128), 0, node_rows)
+            part = pl.ds(step * group, group)
+            hot = one_hot(column_ref[part].reshape(group * edges, 128), 0, node_rows)
             picked_ref[part] = (
                 jnp.dot(hot, rows_ref[...], preferred_element_type=jnp.float32)
                 .astype(jnp.bfloat16)
-                .reshape(OWN, edges, width)
+                .reshape(group, edges, width)
             )
             return carry
 
-        lax.fori_loop(0, blocks // OWN, pick, 0)
+        lax.fori_loop(0, blocks // group, pick, 0)
 
     def plane_parts(layer, columns, hops):
         came = (came_a, came_b)[layer]
@@ -309,13 +317,15 @@
         return total.astype(jnp.bfloat16)
 
     def near_stage(layer, hops):
+        group = group_of(plane_rows * len(hops))
+
         def pick(step, carry):
-            part = pl.ds(step * NEAR, NEAR)
-            columns = column_ref[part].reshape(NEAR * edges, 128)
-            picked_ref[part] += plane_parts(layer, columns, hops).reshape(NEAR, edges, width)
-            return carry
-
-        lax.fori_loop(0, blocks // NEAR, pick, 0)
+            part = pl.ds(step * group, group)
+            columns = column_ref[part].reshape(group * edges, 128)
+            picked_ref[part] += plane_parts(layer, columns, hops).reshape(group, edges, width)
+            return carry
+
+        lax.fori_loop(0, blocks // group, pick, 0)
 
     def block_at(step):
         return jnp.clip(plan_smem[0, step], 0, blocks - 1)
@@ -326,25 +336,21 @@
     def hot_of(block):
         return (place_ids == slot_ref[block]).astype(jnp.float32).astype(jnp.bfloat16)
 
-    def far_stage(layer, hops):
+    def pool_stage(first, count):
         def pool(step, carry):
-            named = [block_at(step * FAR + part) for part in range(FAR)]
-            columns = jnp.concatenate([column_ref[block] for block in named], axis=0)
-            gathered = plane_parts(layer, columns, hops)
-            total = pooled_ref[step * FAR]
-            for part in range(FAR):
-                messages = (
-                    gathered[part * edges : (part + 1) * edges] + picked_ref[named[part]]
+            total = pooled_ref[step * POOL]
+            for part in range(POOL):
+                block = block_at(step * POOL + part)
+                sums = jnp.dot(
+                    hot_of(block), picked_ref[block], preferred_element_type=jnp.float32
                 )
-                sums = jnp.dot(
-                    hot_of(named[part]), messages, preferred_element_type=jnp.float32
-                )
-                keep = plan_smem[1, step * FAR + part].astype(jnp.float32)
+                keep = plan_smem[1, step * POOL + part].astype(jnp.float32)
                 total = total * keep + sums
-                pooled_ref[step * FAR + part + 1] = total
-            return carry
-
-        lax.fori_loop(0, blocks // FAR, pool, 0)
+                pooled_ref[step * POOL + part + 1] = total
+            return carry
+
+        steps = blocks // POOL
+        lax.fori_loop(first * steps // 4, (first + count) * steps // 4, pool, 0)
 
     def degree_stage():
         ones = jnp.ones((edges, 128), jnp.bfloat16)
@@ -361,31 +367,34 @@
 
         lax.fori_loop(0, blocks // COUNT, pool, 0)
 
-        def invert(window, carry):
-            numbers = pooled_ref[last_of(window), :, 0:128]
-            inverse_ref[window] = 1.0 / jnp.maximum(numbers, 1.0)
-            return carry
-
-        lax.fori_loop(0, windows, invert, 0)
+        def invert(step, carry):
+            for part in range(4):
+                window = step * 4 + part
+                numbers = pooled_ref[last_of(window), :, 0:128]
+                inverse_ref[window] = 1.0 / jnp.maximum(numbers, 1.0)
+            return carry
+
+        lax.fori_loop(0, windows // 4, invert, 0)
 
     def mean_stage():
-        def average(window, carry):
-            block = last_of(window)
-            first = pl.multiple_of(window * WIN, WIN)
-            for relation in range(relations):
-                part = slice(relation * WIN, (relation + 1) * WIN)
-                inverse = inverse_ref[window, part, :]
-                for lane in range(0, width, 128):
-                    mean_ref[relation, pl.ds(first, WIN), lane : lane + 128] = (
-                        pooled_ref[block, part, lane : lane + 128] * inverse
-                    ).astype(jnp.bfloat16)
-            return carry
-
-        lax.fori_loop(0, windows, average, 0)
+        def average(step, carry):
+            for window in [step * 4 + part for part in range(4)]:
+                block = last_of(window)
+                first = pl.multiple_of(window * WIN, WIN)
+                for relation in range(relations):
+                    part = slice(relation * WIN, (relation + 1) * WIN)
+                    inverse = inverse_ref[window, part, :]
+                    for lane in range(0, width, 128):
+                        mean_ref[relation, pl.ds(first, WIN), lane : lane + 128] = (
+                            pooled_ref[block, part, lane : lane + 128] * inverse
+                        ).astype(jnp.bfloat16)
+            return carry
+
+        lax.fori_loop(0, windows // 4, average, 0)
 
     def dense_stage(rows_ref, bias_ref, result_ref, last):
         def dense(chunk, carry):
-            rows = pl.ds(pl.multiple_of(chunk * 256, 256), 256)
+            rows = pl.ds(pl.multiple_of(chunk * 512, 512), 512)
             total = bias_ref[...] + jnp.dot(
                 rows_ref[rows, :], weight_ref[relations], preferred_element_type=jnp.float32
             )
@@ -400,47 +409,61 @@
             result_ref[rows, :] = total.astype(jnp.bfloat16)
             return carry
 
-        lax.fori_loop(0, node_rows // 256, dense, 0)
+        lax.fori_loop(0, node_rows // 512, dense, 0)
 
     def source_columns():
         turned = jnp.transpose(source_ref[...].astype(jnp.float32))
+        ones_wide = jnp.ones((2 * edges, 128), jnp.bfloat16)
 
         def spread(group, carry):
             rolled = pltpu.roll(turned, blocks - group * SPREAD, 1)
+            listed = source_ref[pl.ds(pl.multiple_of(group * SPREAD, SPREAD), SPREAD), :]
+            small = listed % 128
+            large = (listed - small).astype(jnp.float32)
+            small = small.astype(jnp.float32)
             for row in range(SPREAD):
-                column_ref[group * SPREAD + row] = jnp.broadcast_to(
-                    rolled[:, row : row + 1], (edges, 128)
-                ).astype(jnp.int32)
+                if row % 2:
+                    column = jnp.broadcast_to(rolled[:, row : row + 1], (edges, 128))
+                else:
+                    diagonal = [
+                        jnp.where(eye, one[row : row + 1, :], 0.0).astype(jnp.bfloat16)
+                        for one in (large, small)
+                    ]
+                    column = jnp.dot(
+                        jnp.concatenate(diagonal, axis=1),
+                        ones_wide,
+                        preferred_element_type=jnp.float32,
+                    )
+                column_ref[group * SPREAD + row] = column.astype(jnp.int32)
             return carry
 
         lax.fori_loop(0, blocks // SPREAD, spread, 0)
 
-    near = [planes // 2, 0] if planes > 2 else list(range(planes))
+    near = [planes // 2]
     far = [hop for hop in range(planes) if hop not in near]
 
     scope = jax.named_scope
     plan_copy = pltpu.make_async_copy(plan_ref, plan_smem, plan_sem)
+    plan_copy.start()
+    pooled_ref[0] = jnp.zeros(pooled_ref.shape[1:], jnp.float32)
     with scope("columns"):
         source_columns()
-    plan_copy.start()
-    pooled_ref[0] = jnp.zeros(pooled_ref.shape[1:], jnp.float32)
     with scope("greeted"):
         pl.semaphore_wait(barrier, devices - 1)
     send_pieces(0, 0)
     with scope("send_a"):
         waiting = send_rows(0, features_ref)
     plan_copy.wait()
+    with scope("compose_b"):
+        compose(bases_b, self_b, coef_b, pieces_b)
     start_plane(0, waiting)
     with scope("degree"):
         degree_stage()
+    with scope("own_a"):
+        own_stage(features_ref)
     with scope("piece_z"):
         land_pieces(0, 0)
     send_pieces(0, 1)
-    with scope("own_a"):
-        own_stage(features_ref)
-    with scope("piece_y"):
-        land_pieces(0, 1)
-    send_pieces(0, 2)
     with scope("land_near_a"):
         for hop in near:
             land_plane(0, hop)
@@ -449,12 +472,19 @@
     with scope("land_far_a"):
         for hop in far:
             land_plane(0, hop)
+    with scope("piece_y"):
+        land_pieces(0, 1)
+    send_pieces(0, 2)
+    send_pieces(1, 0)
+    with scope("far_a"):
+        near_stage(0, far)
+    with scope("pool_a1"):
+        pool_stage(0, 2)
     with scope("piece_x"):
         land_pieces(0, 2)
     send_pieces(0, 3)
-    send_pieces(1, 0)
-    with scope("far_a"):
-        far_stage(0, far)
+    with scope("pool_a2"):
+        pool_stage(2, 2)
     with scope("piece_z_b"):
         land_pieces(1, 0)
     send_pieces(1, 1)
@@ -467,33 +497,35 @@
     with scope("dense_a"):
         dense_stage(features_ref, bias_a, hidden_ref, False)
 
+    with scope("send_b"):
+        waiting = send_rows(1, hidden_ref)
     with scope("piece_y_b"):
         land_pieces(1, 1)
+    start_plane(1, waiting)
     send_pieces(1, 2)
-    with scope("send_b"):
-        waiting = send_rows(1, hidden_ref)
-    start_plane(1, waiting)
     with scope("own_b"):
         own_stage(hidden_ref)
-    with scope("piece_x_b"):
-        land_pieces(1, 2)
-    send_pieces(1, 3)
     with scope("land_near_b"):
         for hop in near:
             land_plane(1, hop)
     with scope("near_b"):
         near_stage(1, near)
+    with scope("piece_x_b"):
+        land_pieces(1, 2)
+    send_pieces(1, 3)
+    with scope("land_far_b"):
+        for hop in far:
+            land_plane(1, hop)
+    with scope("far_b"):
+        near_stage(1, far)
+    with scope("pool_b"):
+        pool_stage(0, 4)
+    with scope("mean_b"):
+        mean_stage()
     with scope("piece_core_b"):
         land_pieces(1, 3)
     with scope("join_b"):
         join_pieces(1)
-    with scope("land_far_b"):
-        for hop in far:
-            land_plane(1, hop)
-    with scope("far_b"):
-        far_stage(1, far)
-    with scope("mean_b"):
-        mean_stage()
     with scope("dense_b"):
         dense_stage(hidden_ref, bias_b, out_ref, True)
 

time: 85.8 us -> 75.1 us (0.88)
  the two profiles are of different devices: /device:TPU:8 before, /device:TPU:0 now
where the time goes in v2:
time: 75.1 us; the launch traced here: 75 us
  Pallas kernels  72.4 us (96%)
  local copies, waits for them, and re-layouts  1.87 us (2%)
    pallas_call x1, Pallas kernels, shards(): pl.pallas_call(functools.partial(fused_kernel, devices), out_shape=jax.Sh...  72.4 us
    unnamed x1, local copies, waits for them, and re-layouts  1.87 us

profile of v2, /device:TPU:0, one launch (start us, length us, event | category | flops | bytes accessed | tf_op | source)
XLA Modules:
  0.0 75.0 jit_solution(11878256473539876342)
XLA Ops:
  0.7 72.4 %rgcn.1 = bf16[1024,256]{1,0:T(8,128)(2,1)} custom-call(s32[128,128]{1,0:T(8,128)} %bitcast.6, s32[128,128]{1,0:T(8,128)} %bitcast.7, s32[128,128]{1,0:T(8,128)} %bitcast.8, s32[32,32]{1,0:T(8,128)} %bitcast.9, s32[1]{0:T(128)S(6)} %copy.16.count_ref, bf16[1024,256]{1,0:T(8,128)(2,1)} %features_ref.1, bf16[30,8,256]{2,1,0:T(8,128)(2,1)} %bases_a.1, ...), custom_call_target="tpu_custom_call" | custom-call | tf_op jit(solution)/shard_map/rgcn/pallas_call | solution.py:570
  73.1 1.9 %copy.17 = bf16[1024,256]{1,0:T(8,128)(2,1)} copy(bf16[1024,256]{1,0:T(8,128)(2,1)} %rgcn.1) | data formatting | bytes 1048576

commit v3 on v2

--- a/solution.py
+++ b/solution.py
@@ -9,7 +9,7 @@
 from jax.sharding import PartitionSpec as P
 
 WIN = 16
-POOL, COUNT, SPREAD = 16, 32, 16
+POOL, COUNT = 32, 32
 VMEM_LIMIT = 63 * 1024 * 1024
 MESH = pl.DeviceIdType.MESH
 
@@ -20,9 +20,9 @@
     return chips // (side * side), side, side, 2
 
 
-def group_of(depth):
+def group_of(depth, devices):
     group = 32
-    while group * depth > 32 * 1024:
+    while group * depth * devices > 1024 * 1024:
         group //= 2
     return group
 
@@ -66,8 +66,8 @@
     sent,
     came_a,
     came_b,
-    hidden_ref,
     plan_ref,
+    turned_ref,
     plan_smem,
     plan_sem,
     send_sems,
@@ -160,7 +160,7 @@
     plan()
 
     slot = relation_ref[...] * WIN + target_ref[...] % WIN
-    slot_ref[...] = jnp.where(row_ids < count_ref[0], slot, -1).reshape(blocks, 1, edges)
+    slot_ref[...] = jnp.where(row_ids < count_ref[0, 0], slot, -1).reshape(blocks, 1, edges)
 
     def copies(layer, stage):
         pieces = (pieces_a, pieces_b)[layer]
@@ -249,7 +249,8 @@
         )
 
     def plane_order():
-        return sorted(range(planes), key=lambda hop: -min(hop, planes - hop))
+        order = sorted(range(planes), key=lambda hop: -min(hop, planes - hop))
+        return order[:1] + [0] * (planes > 1) + order[1:-1]
 
     def pick_plane(layer, rows_ref, hop_z):
         z = lax.rem(my_z + hop_z, planes)
@@ -290,20 +291,34 @@
             waiting = hop_z
         return waiting
 
-    def own_stage(rows_ref):
-        group = group_of(node_rows)
-
-        def pick(step, carry):
-            part = pl.ds(step * group, group)
+    def own_stage(rows_ref, spreading, between=None):
+        group = group_of(node_rows, devices)
+
+        def pick(step, first):
+            part = pl.ds(first, group)
             hot = one_hot(column_ref[part].reshape(group * edges, 128), 0, node_rows)
             picked_ref[part] = (
                 jnp.dot(hot, rows_ref[...], preferred_element_type=jnp.float32)
                 .astype(jnp.bfloat16)
                 .reshape(group, edges, width)
             )
-            return carry
-
-        lax.fori_loop(0, blocks // group, pick, 0)
+
+        if spreading:
+            group = min(group, 16)
+            source_columns(0, group, True)
+            for first in range(0, blocks, group):
+                if first + group < blocks:
+                    source_columns(first + group, group, False)
+                pick(0, first)
+                if between is not None and (first + group) * 4 == blocks * 3:
+                    between()
+        else:
+
+            def body(step, carry):
+                pick(step, step * group)
+                return carry
+
+            lax.fori_loop(0, blocks // group, body, 0)
 
     def plane_parts(layer, columns, hops):
         came = (came_a, came_b)[layer]
@@ -317,7 +332,7 @@
         return total.astype(jnp.bfloat16)
 
     def near_stage(layer, hops):
-        group = group_of(plane_rows * len(hops))
+        group = group_of(plane_rows * len(hops), devices)
 
         def pick(step, carry):
             part = pl.ds(step * group, group)
@@ -411,80 +426,81 @@
 
         lax.fori_loop(0, node_rows // 512, dense, 0)
 
-    def source_columns():
-        turned = jnp.transpose(source_ref[...].astype(jnp.float32))
-        ones_wide = jnp.ones((2 * edges, 128), jnp.bfloat16)
-
-        def spread(group, carry):
-            rolled = pltpu.roll(turned, blocks - group * SPREAD, 1)
-            listed = source_ref[pl.ds(pl.multiple_of(group * SPREAD, SPREAD), SPREAD), :]
-            small = listed % 128
-            large = (listed - small).astype(jnp.float32)
-            small = small.astype(jnp.float32)
-            for row in range(SPREAD):
-                if row % 2:
-                    column = jnp.broadcast_to(rolled[:, row : row + 1], (edges, 128))
-                else:
-                    diagonal = [
-                        jnp.where(eye, one[row : row + 1, :], 0.0).astype(jnp.bfloat16)
-                        for one in (large, small)
-                    ]
-                    column = jnp.dot(
-                        jnp.concatenate(diagonal, axis=1),
-                        ones_wide,
-                        preferred_element_type=jnp.float32,
-                    )
-                column_ref[group * SPREAD + row] = column.astype(jnp.int32)
-            return carry
-
-        lax.fori_loop(0, blocks // SPREAD, spread, 0)
-
-    near = [planes // 2]
-    far = [hop for hop in range(planes) if hop not in near]
+    def source_columns(start, count, mixed):
+        if mixed:
+            ones_wide = jnp.ones((2 * edges, 128), jnp.bfloat16)
+        listed = source_ref[start : start + count, :]
+        turned = turned_ref[...]
+        small = listed % 128
+        large = (listed - small).astype(jnp.float32)
+        small = small.astype(jnp.float32)
+        for row in range(count):
+            if row % 2 or not mixed:
+                column = jnp.broadcast_to(
+                    turned[:, start + row : start + row + 1], (edges, 128)
+                )
+            else:
+                diagonal = [
+                    jnp.where(eye, one[row : row + 1, :], 0.0).astype(jnp.bfloat16)
+                    for one in (large, small)
+                ]
+                column = jnp.dot(
+                    jnp.concatenate(diagonal, axis=1),
+                    ones_wide,
+                    preferred_element_type=jnp.float32,
+                )
+            column_ref[start + row] = column.astype(jnp.int32)
+
+    near = [0]
+    far = [hop for hop in plane_order() if hop not in near]
 
     scope = jax.named_scope
     plan_copy = pltpu.make_async_copy(plan_ref, plan_smem, plan_sem)
     plan_copy.start()
     pooled_ref[0] = jnp.zeros(pooled_ref.shape[1:], jnp.float32)
-    with scope("columns"):
-        source_columns()
+    turned_ref[...] = jnp.transpose(source_ref[...].astype(jnp.float32))
+    plan_copy.wait()
+    with scope("degree"):
+        degree_stage()
     with scope("greeted"):
         pl.semaphore_wait(barrier, devices - 1)
     send_pieces(0, 0)
     with scope("send_a"):
         waiting = send_rows(0, features_ref)
-    plan_copy.wait()
     with scope("compose_b"):
         compose(bases_b, self_b, coef_b, pieces_b)
     start_plane(0, waiting)
-    with scope("degree"):
-        degree_stage()
+
+    def forward():
+        land_pieces(0, 0)
+        send_pieces(0, 1)
+
     with scope("own_a"):
-        own_stage(features_ref)
-    with scope("piece_z"):
-        land_pieces(0, 0)
-    send_pieces(0, 1)
+        own_stage(features_ref, True, forward)
     with scope("land_near_a"):
         for hop in near:
             land_plane(0, hop)
     with scope("near_a"):
         near_stage(0, near)
-    with scope("land_far_a"):
-        for hop in far:
+    with scope("land_mid_a"):
+        for hop in far[:1]:
             land_plane(0, hop)
+    with scope("mid_a"):
+        near_stage(0, far[:1])
     with scope("piece_y"):
         land_pieces(0, 1)
     send_pieces(0, 2)
     send_pieces(1, 0)
+    with scope("land_far_a"):
+        for hop in far[1:]:
+            land_plane(0, hop)
     with scope("far_a"):
-        near_stage(0, far)
-    with scope("pool_a1"):
-        pool_stage(0, 2)
+        near_stage(0, far[1:])
+    with scope("pool_a"):
+        pool_stage(0, 4)
     with scope("piece_x"):
         land_pieces(0, 2)
     send_pieces(0, 3)
-    with scope("pool_a2"):
-        pool_stage(2, 2)
     with scope("piece_z_b"):
         land_pieces(1, 0)
     send_pieces(1, 1)
@@ -495,16 +511,16 @@
     with scope("join_a"):
         join_pieces(0)
     with scope("dense_a"):
-        dense_stage(features_ref, bias_a, hidden_ref, False)
+        dense_stage(features_ref, bias_a, out_ref, False)
 
     with scope("send_b"):
-        waiting = send_rows(1, hidden_ref)
+        waiting = send_rows(1, out_ref)
+    start_plane(1, waiting)
     with scope("piece_y_b"):
         land_pieces(1, 1)
-    start_plane(1, waiting)
     send_pieces(1, 2)
     with scope("own_b"):
-        own_stage(hidden_ref)
+        own_stage(out_ref, False)
     with scope("land_near_b"):
         for hop in near:
             land_plane(1, hop)
@@ -527,7 +543,7 @@
     with scope("join_b"):
         join_pieces(1)
     with scope("dense_b"):
-        dense_stage(hidden_ref, bias_b, out_ref, True)
+        dense_stage(out_ref, bias_b, out_ref, True)
 
 
 def in_smem():
@@ -569,7 +585,7 @@
     most = max(planes, rows_y, rows_x, cores)
     return pl.pallas_call(
         functools.partial(fused_kernel, devices),
-        out_shape=jax.ShapeDtypeStruct((node_rows, width), bf16),
+        out_shape=pltpu.VMEM((node_rows, width), bf16),
         in_specs=[in_vmem()] * 4
         + [in_smem()]
         + [in_vmem()] * 5
@@ -590,8 +606,8 @@
             pltpu.VMEM((came, width), bf16),
             pltpu.VMEM((came, width), bf16),
             pltpu.VMEM((came, width), bf16),
-            pltpu.VMEM((node_rows, width), bf16),
             pltpu.VMEM((8, 128), i32),
+            pltpu.VMEM((edges, blocks), f32),
             pltpu.SMEM((8, 128), i32),
             pltpu.SemaphoreType.DMA,
             pltpu.SemaphoreType.DMA((2, peers)),
@@ -608,7 +624,7 @@
         edge_relation[0],
         edge_target[0],
         send_list[0],
-        block_count,
+        block_count[None],
         features,
         bases_first,
         self_first,

time: 75.1 us -> 70.5 us (0.939)
  Pallas kernels: 72.4 us -> 68.9 us
  local copies, waits for them, and re-layouts: 1.87 us -> 0.8 us
    pallas_call x1, Pallas kernels: 72.4 us -> 68.9 us  [shards(): pl.pallas_call(functools.partial(fused_kernel, devices), out_shape=pltpu....]
    unnamed x1, local copies, waits for them, and re-layouts: 1.87 us -> 0.8 us
where the time goes in v3:
time: 70.5 us; the launch traced here: 70.3 us
  Pallas kernels  68.9 us (98%)
  local copies, waits for them, and re-layouts  0.8 us (1%)
    pallas_call x1, Pallas kernels, shards(): pl.pallas_call(functools.partial(fused_kernel, devices), out_shape=pltpu....  68.9 us

profile of v3, /device:TPU:0, one launch (start us, length us, event | category | flops | bytes accessed | tf_op | source)
XLA Modules:
  0.0 70.3 jit_solution(8597196858765816148)
XLA Ops:
  0.7 68.9 %rgcn.1 = bf16[1024,256]{1,0:T(8,128)(2,1)S(1)} custom-call(s32[128,128]{1,0:T(8,128)} %bitcast.8, s32[128,128]{1,0:T(8,128)} %bitcast.9, s32[128,128]{1,0:T(8,128)} %bitcast.10, s32[32,32]{1,0:T(8,128)} %bitcast.11, s32[1,1]{1,0:T(1,128)} %bitcast.7.count_ref, bf16[1024,256]{1,0:T(8,128)(2,1)} %features_ref.1, bf16[30,8,256]{2,1,0:T(8,128)(2,1)} %bases_a.1, ...), custom_call_target="tpu_custom_call" | custom-call | tf_op jit(solution)/shard_map/rgcn/pallas_call | solution.py:586
  69.5 0.8 %copy.16 = bf16[1024,256]{1,0:T(8,128)(2,1)} copy(bf16[1024,256]{1,0:T(8,128)(2,1)S(1)} %rgcn.1) | data formatting | bytes 1048576

commit v4 on v3

--- a/solution.py
+++ b/solution.py
@@ -252,14 +252,20 @@
         order = sorted(range(planes), key=lambda hop: -min(hop, planes - hop))
         return order[:1] + [0] * (planes > 1) + order[1:-1]
 
-    def pick_plane(layer, rows_ref, hop_z):
-        z = lax.rem(my_z + hop_z, planes)
-        for part in range(plane_rows // 256):
-            first = pl.multiple_of(z * plane_rows + part * 256, 256)
-            hot = one_hot(send_column_ref[pl.ds(first, 256), :], 0, node_rows)
-            sent[pl.ds(first, 256), :] = jnp.dot(
-                hot, rows_ref[...], preferred_element_type=jnp.float32
-            ).astype(jnp.bfloat16)
+    def pick_planes(rows_ref, hops):
+        starts = [
+            pl.multiple_of(lax.rem(my_z + hop, planes) * plane_rows + part * 256, 256)
+            for hop in hops
+            for part in range(plane_rows // 256)
+        ]
+        columns = jnp.concatenate(
+            [send_column_ref[pl.ds(first, 256), :] for first in starts], axis=0
+        )
+        rows = jnp.dot(
+            one_hot(columns, 0, node_rows), rows_ref[...], preferred_element_type=jnp.float32
+        ).astype(jnp.bfloat16)
+        for part, first in enumerate(starts):
+            sent[pl.ds(first, 256), :] = rows[part * 256 : (part + 1) * 256]
 
     def start_plane(layer, hop_z):
         def start(hop_low, carry):
@@ -283,12 +289,13 @@
         came[pl.ds(pl.multiple_of(me * slots, slots), slots), :] = jnp.zeros(
             (slots, width), jnp.bfloat16
         )
-        waiting = None
-        for hop_z in plane_order():
-            pick_plane(layer, rows_ref, hop_z)
-            if waiting is not None:
-                start_plane(layer, waiting)
-            waiting = hop_z
+        waiting = []
+        hops = plane_order()
+        for first in range(0, planes, 2):
+            pick_planes(rows_ref, hops[first : first + 2])
+            for hop in waiting:
+                start_plane(layer, hop)
+            waiting = hops[first : first + 2]
         return waiting
 
     def own_stage(rows_ref, spreading, between=None):
@@ -408,8 +415,10 @@
         lax.fori_loop(0, windows // 4, average, 0)
 
     def dense_stage(rows_ref, bias_ref, result_ref, last):
+        height = min(node_rows, 1024 if last else 512)
+
         def dense(chunk, carry):
-            rows = pl.ds(pl.multiple_of(chunk * 512, 512), 512)
+            rows = pl.ds(pl.multiple_of(chunk * height, height), height)
             total = bias_ref[...] + jnp.dot(
                 rows_ref[rows, :], weight_ref[relations], preferred_element_type=jnp.float32
             )
@@ -424,7 +433,7 @@
             result_ref[rows, :] = total.astype(jnp.bfloat16)
             return carry
 
-        lax.fori_loop(0, node_rows // 512, dense, 0)
+        lax.fori_loop(0, node_rows // height, dense, 0)
 
     def source_columns(start, count, mixed):
         if mixed:
@@ -469,7 +478,8 @@
         waiting = send_rows(0, features_ref)
     with scope("compose_b"):
         compose(bases_b, self_b, coef_b, pieces_b)
-    start_plane(0, waiting)
+    for hop in waiting:
+        start_plane(0, hop)
 
     def forward():
         land_pieces(0, 0)
@@ -482,25 +492,25 @@
             land_plane(0, hop)
     with scope("near_a"):
         near_stage(0, near)
+    with scope("piece_y"):
+        land_pieces(0, 1)
+    send_pieces(0, 2)
+    send_pieces(1, 0)
     with scope("land_mid_a"):
         for hop in far[:1]:
             land_plane(0, hop)
     with scope("mid_a"):
         near_stage(0, far[:1])
-    with scope("piece_y"):
-        land_pieces(0, 1)
-    send_pieces(0, 2)
-    send_pieces(1, 0)
     with scope("land_far_a"):
         for hop in far[1:]:
             land_plane(0, hop)
     with scope("far_a"):
         near_stage(0, far[1:])
-    with scope("pool_a"):
-        pool_stage(0, 4)
     with scope("piece_x"):
         land_pieces(0, 2)
     send_pieces(0, 3)
+    with scope("pool_a"):
+        pool_stage(0, 4)
     with scope("piece_z_b"):
         land_pieces(1, 0)
     send_pieces(1, 1)
@@ -515,7 +525,8 @@
 
     with scope("send_b"):
         waiting = send_rows(1, out_ref)
-    start_plane(1, waiting)
+    for hop in waiting:
+        start_plane(1, hop)
     with scope("piece_y_b"):
         land_pieces(1, 1)
     send_pieces(1, 2)
@@ -526,14 +537,14 @@
             land_plane(1, hop)
     with scope("near_b"):
         near_stage(1, near)
-    with scope("piece_x_b"):
-        land_pieces(1, 2)
-    send_pieces(1, 3)
     with scope("land_far_b"):
         for hop in far:
             land_plane(1, hop)
     with scope("far_b"):
         near_stage(1, far)
+    with scope("piece_x_b"):
+        land_pieces(1, 2)
+    send_pieces(1, 3)
     with scope("pool_b"):
         pool_stage(0, 4)
     with scope("mean_b"):

time: 70.5 us -> 69 us (0.979)
  Pallas kernels: 68.9 us -> 67.4 us
    pallas_call x1, Pallas kernels: 68.9 us -> 67.4 us  [shards(): pl.pallas_call(functools.partial(fused_kernel, devices), out_shape=pltpu....]
where the time goes in v4:
time: 69 us; the launch traced here: 68.8 us
  Pallas kernels  67.4 us (98%)
  local copies, waits for them, and re-layouts  0.8 us (1%)
    pallas_call x1, Pallas kernels, shards(): pl.pallas_call(functools.partial(fused_kernel, devices), out_shape=pltpu....  67.4 us

profile of v4, /device:TPU:0, one launch (start us, length us, event | category | flops | bytes accessed | tf_op | source)
XLA Modules:
  0.0 68.8 jit_solution(10994501422184974996)
XLA Ops:
  0.7 67.4 %rgcn.1 = bf16[1024,256]{1,0:T(8,128)(2,1)S(1)} custom-call(s32[128,128]{1,0:T(8,128)} %bitcast.8, s32[128,128]{1,0:T(8,128)} %bitcast.9, s32[128,128]{1,0:T(8,128)} %bitcast.10, s32[32,32]{1,0:T(8,128)} %bitcast.11, s32[1,1]{1,0:T(1,128)} %bitcast.7.count_ref, bf16[1024,256]{1,0:T(8,128)(2,1)} %features_ref.1, bf16[30,8,256]{2,1,0:T(8,128)(2,1)} %bases_a.1, ...), custom_call_target="tpu_custom_call" | custom-call | tf_op jit(solution)/shard_map/rgcn/pallas_call | solution.py:597
  68.0 0.8 %copy.16 = bf16[1024,256]{1,0:T(8,128)(2,1)} copy(bf16[1024,256]{1,0:T(8,128)(2,1)S(1)} %rgcn.1) | data formatting | bytes 1048576

commit v5 on v4

--- a/solution.py
+++ b/solution.py
@@ -527,11 +527,11 @@
         waiting = send_rows(1, out_ref)
     for hop in waiting:
         start_plane(1, hop)
+    with scope("own_b"):
+        own_stage(out_ref, False)
     with scope("piece_y_b"):
         land_pieces(1, 1)
     send_pieces(1, 2)
-    with scope("own_b"):
-        own_stage(out_ref, False)
     with scope("land_near_b"):
         for hop in near:
             land_plane(1, hop)

time: 69 us -> 67.7 us (0.981)
  Pallas kernels: 67.4 us -> 66.1 us
    pallas_call x1, Pallas kernels: 67.4 us -> 66.1 us  [shards(): pl.pallas_call(functools.partial(fused_kernel, devices), out_shape=pltpu....]
where the time goes in v5:
time: 67.7 us; the launch traced here: 67.6 us
  Pallas kernels  66.1 us (98%)
  local copies, waits for them, and re-layouts  0.8 us (1%)
    pallas_call x1, Pallas kernels, shards(): pl.pallas_call(functools.partial(fused_kernel, devices), out_shape=pltpu....  66.1 us

profile of v5, /device:TPU:0, one launch (start us, length us, event | category | flops | bytes accessed | tf_op | source)
XLA Modules:
  0.0 67.6 jit_solution(17933900005020405724)
XLA Ops:
  0.7 66.1 %rgcn.1 = bf16[1024,256]{1,0:T(8,128)(2,1)S(1)} custom-call(s32[128,128]{1,0:T(8,128)} %bitcast.8, s32[128,128]{1,0:T(8,128)} %bitcast.9, s32[128,128]{1,0:T(8,128)} %bitcast.10, s32[32,32]{1,0:T(8,128)} %bitcast.11, s32[1,1]{1,0:T(1,128)} %bitcast.7.count_ref, bf16[1024,256]{1,0:T(8,128)(2,1)} %features_ref.1, bf16[30,8,256]{2,1,0:T(8,128)(2,1)} %bases_a.1, ...), custom_call_target="tpu_custom_call" | custom-call | tf_op jit(solution)/shard_map/rgcn/pallas_call | solution.py:597
  66.8 0.8 %copy.16 = bf16[1024,256]{1,0:T(8,128)(2,1)} copy(bf16[1024,256]{1,0:T(8,128)(2,1)S(1)} %rgcn.1) | data formatting | bytes 1048576
